TPU v7x, 32 devices: a whole 2x2x4 slice. The times are simulated.
32 devices in a mesh: ga: 8 (over z, x), band: 4 (over y, core).
Axes of the slice: x: 2, y: 2, z: 4, core: 2. Of those that a mesh axis runs over, the one named last changes fastest.
Arguments:
- coeffs: bfloat16 [2, 512, 40960], P(None, ('ga', 'band')), may hold values from -6 to 6
- projectors: bfloat16 [1280, 2, 40960], P(None, None, 'ga'), may hold values from -0.01953125 to 0.01953125
- block_coupling: float32 [1280, 18], replicated, may hold values from -12 to 12
- atom_counts: int32 [160], replicated, may hold values from 4 to 18, as said below
- wave_counts: int32 [8], P('ga'), may hold values from 3840 to 5120
Outputs:
- applied: bfloat16 [2, 512, 40960], P(None, ('ga', 'band'))
- band_energy: float32 [512], P(('ga', 'band'))
- total_energy: float32 [], replicated
Inputs may be any that keep to these rules, and one draw needn't show every extreme that they name: `atom_counts`: each atom has 4, 8 or 18 projectors, the counts sum to 1280 and the largest is 18.
All inputs are finite; a program needn't handle non-finite values.
Results may differ from a plain program's by a relative error of at most 0.013.
Values may be sent and summed in bfloat16 or wider, within the bound.
A program may use at most 128 MiB of HBM per device.

v0:
```python
import math
import jax
import jax.numpy as jnp
from jax import lax
from jax.sharding import PartitionSpec as P


def block_tables(atom_counts, row_ids):
    atom_ends = jnp.cumsum(atom_counts)
    atom_starts = atom_ends - atom_counts
    inside = (atom_starts[None, :] <= row_ids[:, None]) & (atom_ends[None, :] > row_ids[:, None])
    block_first = jnp.sum(jnp.where(inside, atom_starts[None, :], 0), axis=1)
    block_length = jnp.sum(jnp.where(inside, atom_counts[None, :], 0), axis=1)
    return (block_first, block_length)


def coupling_matrix(block_first, block_length, coupling_rows, column_count):
    column_ids = lax.iota(jnp.int32, column_count)
    offsets = column_ids[None, :] - block_first[:, None]
    matrix = jnp.zeros((coupling_rows.shape[0], column_count), jnp.float32)
    for offset in range(coupling_rows.shape[1]):
        hit = (offsets == offset) & (offset < block_length[:, None])
        matrix = jnp.where(hit, coupling_rows[:, offset : offset + 1], matrix)
    return matrix


def shards(coeffs, projectors, block_coupling, atom_counts, wave_counts):
    moved_bands = lax.all_to_all(coeffs, "ga", split_axis=2, concat_axis=1, tiled=True)
    own_bands = coeffs.shape[1]
    group_bands = moved_bands.shape[1]
    wave_slots = projectors.shape[2]
    proj_total_rows = projectors.shape[0]
    in_sphere = (lax.iota(jnp.int32, wave_slots) < wave_counts[0]).astype(jnp.float32)
    masked = moved_bands * in_sphere.astype(jnp.bfloat16)
    real_part = masked[0]
    imag_part = masked[1]
    stacked = jnp.concatenate(
        [jnp.concatenate([real_part, imag_part], 1), jnp.concatenate([imag_part, -real_part], 1)], 0
    )
    flat_beta = projectors.reshape(proj_total_rows, 2 * wave_slots)
    contract_last = (((1,), (1,)), ((), ()))
    contract_first = (((0,), (0,)), ((), ()))
    ga_index = lax.axis_index("ga")
    local_terms = lax.dot_general(
        flat_beta, stacked, contract_last, preferred_element_type=jnp.float32
    )
    projections = lax.psum(local_terms, "ga")
    block_first, block_length = block_tables(atom_counts, lax.iota(jnp.int32, proj_total_rows))
    matrix = coupling_matrix(block_first, block_length, block_coupling, proj_total_rows)
    coupled = jnp.dot(
        matrix, projections, precision=lax.Precision.HIGHEST, preferred_element_type=jnp.float32
    )
    energy_terms = jnp.sum(projections * coupled, axis=0)
    group_energy = (energy_terms[:group_bands] + energy_terms[group_bands:]) / proj_total_rows
    band_energy = lax.dynamic_slice_in_dim(group_energy, ga_index * own_bands, own_bands, 0)
    total_energy = lax.psum(jnp.sum(group_energy), "band")
    products = lax.dot_general(
        coupled.astype(jnp.bfloat16), flat_beta, contract_first, preferred_element_type=jnp.float32
    )
    band_total = own_bands * lax.axis_size("ga") * lax.axis_size("band")
    total_energy = total_energy / math.sqrt(band_total)
    real_out = products[:group_bands, :wave_slots] - products[group_bands:, wave_slots:]
    imag_out = products[:group_bands, wave_slots:] + products[group_bands:, :wave_slots]
    result = (jnp.stack([real_out, imag_out]) * in_sphere).astype(jnp.bfloat16)
    applied = lax.all_to_all(result, "ga", split_axis=1, concat_axis=2, tiled=True)
    return (applied, band_energy, total_energy)


def solution(mesh):
    placed = (P(None, ("ga", "band"), None), P(None, None, "ga"), P(), P(), P("ga"))
    return jax.shard_map(
        shards,
        mesh=mesh,
        in_specs=placed,
        out_specs=(P(None, ("ga", "band"), None), P(("ga", "band")), P()),
        check_vma=False,
    )
```

profile of v0, /device:TPU:0, one launch (start us, length us, event | category | flops | bytes accessed | tf_op | source)
XLA Modules:
  0.0 439.4 jit_solution(13984395675737779399)
XLA Ops:
  7.2 38.0 %copy.21 = bf16[2,16,40960]{1,0,2:T(2,128)(2,1)} copy(bf16[2,16,40960]{2,1,0:T(8,128)(2,1)} %param.5) | data formatting | bytes 5242880 | tf_op args[0]
  45.1 24.1 %reshape.129 = bf16[8,2,81920]{2,1,0:T(2,128)(2,1)} reshape(bf16[40960,2,16]{2,1,0:T(2,128)(2,1)} %bitcast.40) | data formatting | bytes 5242880
  69.2 7.3 %all-to-all-start = ((bf16[8,2,81920]{2,1,0:T(2,128)(2,1)}), bf16[8,2,81920]{2,1,0:T(2,128)(2,1)S(1)}, u32[]{:S(2)}, u32[]{:S(2)}) async-start(bf16[8,2,81920]{2,1,0:T(2,128)(2,1)} %reshape.129), calls=%async_computation | async-start | bytes 5242880 | tf_op jit(solution)/shard_map/all_to_all | solution.py:28
  76.5 0.4 all-reduce.3.cloned.1.call-start
  77.6 23.8 %copy.29 = bf16[160,8,2,5120]{3,1,2,0:T(8,128)(2,1)} copy(bf16[160,8,2,5120]{3,2,1,0:T(2,128)(2,1)} %bitcast.41) | data formatting | bytes 52428800
  101.3 34.6 %all-to-all-done = bf16[8,2,81920]{2,1,0:T(2,128)(2,1)S(1)} async-done(((bf16[8,2,81920]{2,1,0:T(2,128)(2,1)}), bf16[8,2,81920]{2,1,0:T(2,128)(2,1)S(1)}, u32[]{:S(2)}, u32[]{:S(2)}) %all-to-all-start) | async-done | bytes 2621472 | tf_op jit(solution)/shard_map/all_to_all | solution.py:28
  136.0 17.1 %reshape.130 = bf16[40960,2,16]{2,1,0:T(2,128)(2,1)} reshape(bf16[8,2,81920]{2,1,0:T(2,128)(2,1)S(1)} %all-to-all-done) | data formatting | bytes 5242880
  153.0 37.5 %copy.28 = bf16[2,16,8,5120]{3,1,2,0:T(8,128)(2,1)S(1)} copy(bf16[2,16,8,5120]{1,0,3,2:T(2,128)(2,1)} %bitcast.39) | data formatting | bytes 5242880 | tf_op jit(solution)/shard_map/all_to_all | solution.py:28
  191.2 28.8 %fusion.138 = f32[1280,256]{0,1:T(8,128)} fusion(bf16[1280,10240]{1,0:T(8,128)(2,1)} %bitcast.37, bf16[128,5120]{1,0:T(8,128)(2,1)S(1)} %fusion.168, bf16[128,5120]{1,0:T(8,128)(2,1)S(1)} %get-tuple-element.28, bf16[128,5120]{1,0:T(8,128)(2,1)S(1)} %get-tuple-element.27), kind=kOutput, calls=%fused_computation.122 | convolution fusion | flops 6731857920 | bytes 31457280 | tf_op jit(solution)/shard_map/dot_general | solution.py:44
  221.3 81.6 %all-reduce.3.cloned.1.call-done = f32[1280,256]{0,1:T(8,128)} async-done(((f32[1280,256]{0,1:T(8,128)}), f32[1280,256]{0,1:T(8,128)}) %all-reduce.3.cloned.1.call-update) | async-done | bytes 1310736 | tf_op jit(solution)/shard_map/psum | solution.py:47
  303.0 39.1 %fusion = f32[1280,256]{1,0:T(8,128)} fusion(f32[1280,256]{0,1:T(8,128)} %all-reduce.3.cloned.1.call-done, f32[1280]{0:T(1024)S(1)} %get-tuple-element.19, f32[1280]{0:T(1024)S(1)} %get-tuple-element.20, f32[1280]{0:T(1024)S(1)} %get-tuple-element.4, f32[1280]{0:T(1024)S(1)} %get-tuple-element.5, f32[1280]{0:T(1024)S(1)} %get-tuple-element.6, ...), kind=kOutput, calls=%fused_computation | convolution fusion | flops 5123276800 | bytes 2741760 | tf_op jit(solution)/shard_map/dot_general | solution.py:50
  342.1 13.0 %fusion.144 = f32[256,10240]{1,0:T(8,128)S(1)} fusion(bf16[1280,10240]{1,0:T(8,128)(2,1)} %bitcast.38, f32[1280,256]{1,0:T(8,128)} %fusion), kind=kOutput, calls=%fused_computation.136 | convolution fusion | flops 6711214080 | bytes 38010880 | tf_op jit(solution)/shard_map/dot_general | solution.py:57
  355.1 0.8 fusion.142
  355.9 0.5 fusion.81
  356.4 4.2 copy.24
  360.6 3.7 all-to-all-start.1
  364.2 2.8 copy.26
  367.0 1.9 multiply_reduce_fusion
  368.9 0.6 fusion.169
  369.5 7.3 %psum.15 = f32[]{:T(128)} all-reduce(f32[]{:T(128)} %get-tuple-element.23), channel_id=1, replica_groups=mesh['ga'=8,'band'=4] {'band'}, use_global_device_ids=true, to_apply=%region_7.8 | all-reduce | flops 1 | bytes 8 | tf_op jit(solution)/shard_map/psum | solution.py:56
  376.9 0.6 dynamic_slice.3
  378.1 45.7 %all-to-all-done.1 = bf16[2,128,5120]{2,0,1:T(2,128)(2,1)S(1)} async-done(((bf16[2,128,5120]{2,0,1:T(2,128)(2,1)}), bf16[2,128,5120]{2,0,1:T(2,128)(2,1)S(1)}, u32[]{:S(2)}, u32[]{:S(2)}) %all-to-all-start.1) | async-done | bytes 2621472 | tf_op jit(solution)/shard_map/all_to_all | solution.py:65
  423.8 2.9 copy.25
  426.7 4.5 %all_to_all.33 = bf16[2,16,40960]{2,1,0:T(8,128)(2,1)} reshape(bf16[2,16,8,5120]{3,2,1,0:T(8,128)(2,1)} %copy.25) | data formatting | bytes 5242880 | tf_op jit(solution)/shard_map/all_to_all | solution.py:65
  (19 shorter events, 1.9 us)
Async XLA Ops:
  69.2 66.8 %all-to-all-start = ((bf16[8,2,81920]{2,1,0:T(2,128)(2,1)}), bf16[8,2,81920]{2,1,0:T(2,128)(2,1)S(1)}, u32[]{:S(2)}, u32[]{:S(2)}) async-start(bf16[8,2,81920]{2,1,0:T(2,128)(2,1)} %reshape.129), calls=%async_computation | async-start | bytes 5242880 | tf_op jit(solution)/shard_map/all_to_all | solution.py:28
  76.5 226.5 %all-reduce.3.cloned.1.call-start = ((), (), s32[]{:S(2)}) async-start(), calls=%async_computation.2 | async-start | bytes 2621440 | tf_op jit(solution)/shard_map/psum | solution.py:47
  191.2 28.9 %copy-start.1 = (s32[160]{0:T(256)S(1)}, s32[160]{0:T(256)}, u32[]{:S(2)}) copy-start(s32[160]{0:T(256)} %param.8) | copy-start | bytes 1924
  191.2 29.4 %copy-start = (f32[1280,18]{0,1:T(8,128)S(1)}, f32[1280,18]{0,1:T(8,128)}, u32[]{:S(2)}) copy-start(f32[1280,18]{0,1:T(8,128)} %param.7) | copy-start | bytes 276484
  360.6 63.2 %all-to-all-start.1 = ((bf16[2,128,5120]{2,0,1:T(2,128)(2,1)}), bf16[2,128,5120]{2,0,1:T(2,128)(2,1)S(1)}, u32[]{:S(2)}, u32[]{:S(2)}) async-start(bf16[2,128,5120]{2,0,1:T(2,128)(2,1)} %copy.24), calls=%async_computation.1 | async-start | bytes 5242880 | tf_op jit(solution)/shard_map/all_to_all | solution.py:65
Sparse Core Ops, SparseCore 0:
  220.2 82.7 all-reduce.2
where the time goes:
time: 447 us; the launch traced here: 439 us
  waiting for transfers between devices  162 us (36%)
  local copies, waits for them, and re-layouts  156 us (35%)
  matrix products  81 us (18%)
  between operations  16.8 us (4%)
  starting transfers between devices  11.4 us (3%)
  blocking collectives  7.33 us (2%)
  other arithmetic  4.94 us (1%)
    unnamed x8, local copies, waits for them, and re-layouts  103 us
    psum x1, waiting for transfers between devices, shards(): projections = lax.psum(local_terms, 'ga')  81.6 us
    all_to_all x1, waiting for transfers between devices, shards(): lax.all_to_all(result, 'ga', split_axis=1, concat_axis=2, tiled=True)  45.7 us
    dot_general x1, matrix products, shards(): jnp.dot(matrix, projections, precision=lax.Precision.HIGHEST, preferred_e...  39.1 us
    all_to_all x1, local copies, waits for them, and re-layouts, shards(): lax.all_to_all(coeffs, 'ga', split_axis=2, concat_axis=1, tiled=True)  37.5 us
    all_to_all x1, waiting for transfers between devices, shards(): lax.all_to_all(coeffs, 'ga', split_axis=2, concat_axis=1, tiled=True)  34.6 us
    dot_general x1, matrix products, shards(): lax.dot_general(flat_beta, stacked, contract_last, preferred_element_type...  28.8 us
    dot_general x1, matrix products, shards(): lax.dot_general(coupled.astype(jnp.bfloat16), flat_beta, contract_first,...  13 us
  transfers between devices with their start and end apart: 3, of which 3 were waited for; matrix products, arithmetic and copies ran while one was open for 7% of the time, Pallas kernels for 0%

commit v1 on v0

--- a/solution.py
+++ b/solution.py
@@ -62,7 +62,10 @@
     real_out = products[:group_bands, :wave_slots] - products[group_bands:, wave_slots:]
     imag_out = products[:group_bands, wave_slots:] + products[group_bands:, :wave_slots]
     result = (jnp.stack([real_out, imag_out]) * in_sphere).astype(jnp.bfloat16)
-    applied = lax.all_to_all(result, "ga", split_axis=1, concat_axis=2, tiled=True)
+    devices = lax.axis_size("ga")
+    shards_2 = jnp.stack(jnp.split(result, devices, axis=1), axis=0)
+    shards_2 = lax.all_to_all(shards_2, "ga", split_axis=0, concat_axis=0)
+    applied = jnp.concatenate(shards_2, axis=2)
     return (applied, band_energy, total_energy)
 
 

time: 447 us -> 430 us (0.962)
  matrix products: 81 us -> 71.2 us
    dot_general x1, matrix products: 39.1 us -> 29.3 us  [shards(): jnp.dot(matrix, projections, precision=lax.Precision.HIGHEST, preferred_e...]
    all_to_all x2 -> x0, local copies, waits for them, and re-layouts: 7.43 us -> none  [shards(): lax.all_to_all(result, 'ga', split_axis=1, concat_axis=2, tiled=True)]
    unnamed x8 -> x15, local copies, waits for them, and re-layouts: 103 us -> 108 us
where the time goes in v1:
time: 430 us; the launch traced here: 425 us
  waiting for transfers between devices  162 us (38%)
  local copies, waits for them, and re-layouts  152 us (35%)
  matrix products  71.2 us (17%)
  between operations  16.6 us (4%)
  starting transfers between devices  11.2 us (3%)
  blocking collectives  7.34 us (2%)
  other arithmetic  4.95 us (1%)
    unnamed x15, local copies, waits for them, and re-layouts  108 us
    psum x1, waiting for transfers between devices, shards(): projections = lax.psum(local_terms, 'ga')  81.6 us
    all_to_all x1, waiting for transfers between devices, shards(): shards_2 = lax.all_to_all(shards_2, 'ga', split_axis=0, concat_axis=0)  45.7 us
    all_to_all x1, local copies, waits for them, and re-layouts, shards(): lax.all_to_all(coeffs, 'ga', split_axis=2, concat_axis=1, tiled=True)  37.5 us
    all_to_all x1, waiting for transfers between devices, shards(): lax.all_to_all(coeffs, 'ga', split_axis=2, concat_axis=1, tiled=True)  34.8 us
    dot_general x1, matrix products, shards(): jnp.dot(matrix, projections, precision=lax.Precision.HIGHEST, preferred_e...  29.3 us
    dot_general x1, matrix products, shards(): lax.dot_general(flat_beta, stacked, contract_last, preferred_element_type...  28.8 us
    dot_general x1, matrix products, shards(): lax.dot_general(coupled.astype(jnp.bfloat16), flat_beta, contract_first,...  13 us
  transfers between devices with their start and end apart: 3, of which 3 were waited for; matrix products, arithmetic and copies ran while one was open for 7% of the time, Pallas kernels for 0%

profile of v1, /device:TPU:0, one launch (start us, length us, event | category | flops | bytes accessed | tf_op | source)
XLA Modules:
  0.0 425.4 jit_solution(17539805202780796367)
XLA Ops:
  7.2 38.0 %copy.19 = bf16[2,16,40960]{1,0,2:T(2,128)(2,1)} copy(bf16[2,16,40960]{2,1,0:T(8,128)(2,1)} %param.5) | data formatting | bytes 5242880 | tf_op args[0]
  45.1 24.1 %reshape.137 = bf16[8,2,81920]{2,1,0:T(2,128)(2,1)} reshape(bf16[40960,2,16]{2,1,0:T(2,128)(2,1)} %bitcast.70) | data formatting | bytes 5242880
  69.2 7.3 %all-to-all-start = ((bf16[8,2,81920]{2,1,0:T(2,128)(2,1)}), bf16[8,2,81920]{2,1,0:T(2,128)(2,1)S(1)}, u32[]{:S(2)}, u32[]{:S(2)}) async-start(bf16[8,2,81920]{2,1,0:T(2,128)(2,1)} %reshape.137), calls=%async_computation | async-start | bytes 5242880 | tf_op jit(solution)/shard_map/all_to_all | solution.py:28
  77.4 23.8 %copy.27 = bf16[160,8,2,5120]{3,1,2,0:T(8,128)(2,1)} copy(bf16[160,8,2,5120]{3,2,1,0:T(2,128)(2,1)} %bitcast.71) | data formatting | bytes 52428800
  101.2 34.8 %all-to-all-done = bf16[8,2,81920]{2,1,0:T(2,128)(2,1)S(1)} async-done(((bf16[8,2,81920]{2,1,0:T(2,128)(2,1)}), bf16[8,2,81920]{2,1,0:T(2,128)(2,1)S(1)}, u32[]{:S(2)}, u32[]{:S(2)}) %all-to-all-start) | async-done | bytes 2621472 | tf_op jit(solution)/shard_map/all_to_all | solution.py:28
  136.0 17.1 %reshape.138 = bf16[40960,2,16]{2,1,0:T(2,128)(2,1)} reshape(bf16[8,2,81920]{2,1,0:T(2,128)(2,1)S(1)} %all-to-all-done) | data formatting | bytes 5242880
  153.0 37.5 %copy.25 = bf16[2,16,8,5120]{3,1,2,0:T(8,128)(2,1)S(1)} copy(bf16[2,16,8,5120]{1,0,3,2:T(2,128)(2,1)} %bitcast.69) | data formatting | bytes 5242880 | tf_op jit(solution)/shard_map/all_to_all | solution.py:28
  191.2 28.8 %fusion.138 = f32[1280,256]{0,1:T(8,128)} fusion(bf16[1280,10240]{1,0:T(8,128)(2,1)} %bitcast.67, bf16[128,5120]{1,0:T(8,128)(2,1)S(1)} %fusion.176, bf16[128,5120]{1,0:T(8,128)(2,1)S(1)} %get-tuple-element.28, bf16[128,5120]{1,0:T(8,128)(2,1)S(1)} %get-tuple-element.27), kind=kOutput, calls=%fused_computation.122 | convolution fusion | flops 6731857920 | bytes 31457280 | tf_op jit(solution)/shard_map/dot_general | solution.py:44
  221.3 81.6 %all-reduce.3.cloned.1.call-done = f32[1280,256]{0,1:T(8,128)} async-done(((f32[1280,256]{0,1:T(8,128)}), f32[1280,256]{0,1:T(8,128)}) %all-reduce.3.cloned.1.call-update) | async-done | bytes 1310736 | tf_op jit(solution)/shard_map/psum | solution.py:47
  303.0 29.3 %fusion = f32[1280,256]{1,0:T(8,128)} fusion(f32[1280,256]{0,1:T(8,128)} %all-reduce.3.cloned.1.call-done, f32[1280]{0:T(1024)S(1)} %get-tuple-element.19, f32[1280]{0:T(1024)S(1)} %get-tuple-element.20, f32[1280]{0:T(1024)S(1)} %get-tuple-element.4, f32[1280]{0:T(1024)S(1)} %get-tuple-element.5, f32[1280]{0:T(1024)S(1)} %get-tuple-element.6, ...), kind=kOutput, calls=%fused_computation | convolution fusion | flops 5123276800 | bytes 2741760 | tf_op jit(solution)/shard_map/dot_general | solution.py:50
  332.3 13.0 %fusion.144 = f32[256,10240]{1,0:T(8,128)S(1)} fusion(bf16[1280,10240]{1,0:T(8,128)(2,1)} %bitcast.68, f32[1280,256]{1,0:T(8,128)} %fusion), kind=kOutput, calls=%fused_computation.136 | convolution fusion | flops 6711214080 | bytes 38010880 | tf_op jit(solution)/shard_map/dot_general | solution.py:57
  345.3 0.8 fusion.142
  346.5 0.7 fusion.153
  347.3 0.7 fusion.152
  348.0 0.7 fusion.151
  348.8 0.7 fusion.150
  349.5 0.7 fusion.149
  350.3 0.7 fusion.148
  352.5 3.7 all-to-all-start.1
  356.2 2.8 copy.23
  359.0 1.9 multiply_reduce_fusion
  361.5 7.3 %psum.15 = f32[]{:T(128)} all-reduce(f32[]{:T(128)} %get-tuple-element.23), channel_id=1, replica_groups=mesh['ga'=8,'band'=4] {'band'}, use_global_device_ids=true, to_apply=%region_7.8 | all-reduce | flops 1 | bytes 8 | tf_op jit(solution)/shard_map/psum | solution.py:56
  370.1 45.7 %all-to-all-done.1 = bf16[8,2,16,5120]{3,2,1,0:T(8,128)(2,1)S(1)} async-done(((bf16[8,2,16,5120]{3,2,1,0:T(8,128)(2,1)}), bf16[8,2,16,5120]{3,2,1,0:T(8,128)(2,1)S(1)}, u32[]{:S(2)}, u32[]{:S(2)}) %all-to-all-start.1) | async-done | bytes 2621472 | tf_op jit(solution)/shard_map/all_to_all | solution.py:67
  415.7 1.7 copy.26
  (25 shorter events, 5.2 us)
Async XLA Ops:
  69.2 66.8 %all-to-all-start = ((bf16[8,2,81920]{2,1,0:T(2,128)(2,1)}), bf16[8,2,81920]{2,1,0:T(2,128)(2,1)S(1)}, u32[]{:S(2)}, u32[]{:S(2)}) async-start(bf16[8,2,81920]{2,1,0:T(2,128)(2,1)} %reshape.137), calls=%async_computation | async-start | bytes 5242880 | tf_op jit(solution)/shard_map/all_to_all | solution.py:28
  76.5 226.5 %all-reduce.3.cloned.1.call-start = ((), (), s32[]{:S(2)}) async-start(), calls=%async_computation.2 | async-start | bytes 2621440 | tf_op jit(solution)/shard_map/psum | solution.py:47
  191.2 28.9 %copy-start.1 = (s32[160]{0:T(256)S(1)}, s32[160]{0:T(256)}, u32[]{:S(2)}) copy-start(s32[160]{0:T(256)} %param.8) | copy-start | bytes 1924
  191.2 29.4 %copy-start = (f32[1280,18]{0,1:T(8,128)S(1)}, f32[1280,18]{0,1:T(8,128)}, u32[]{:S(2)}) copy-start(f32[1280,18]{0,1:T(8,128)} %param.7) | copy-start | bytes 276484
  352.5 63.2 %all-to-all-start.1 = ((bf16[8,2,16,5120]{3,2,1,0:T(8,128)(2,1)}), bf16[8,2,16,5120]{3,2,1,0:T(8,128)(2,1)S(1)}, u32[]{:S(2)}, u32[]{:S(2)}) async-start(bf16[8,2,16,5120]{3,2,1,0:T(8,128)(2,1)} %fusion.146), calls=%async_computation.1 | async-start | bytes 5242880 | tf_op jit(solution)/shard_map/all_to_all | solution.py:67
Sparse Core Ops, SparseCore 0:
  220.2 82.7 all-reduce.2
